TPU v7x, 32 devices: a whole 2x2x4 slice. The times are simulated.
32 devices in a mesh: gx: 2 (over x), gy: 4 (over y, core), gz: 4 (over z).
Axes of the slice: x: 2, y: 2, z: 4, core: 2. Of those that a mesh axis runs over, the one named last changes fastest.
Arguments:
- metric_pert: float32 [6, 32, 64, 512], P(None, 'gx', 'gy', 'gz'), may hold values from -1.8 to 1.8
- curvature: float32 [6, 32, 64, 512], P(None, 'gx', 'gy', 'gz'), may hold values from -6 to 6
- interp_weights: bfloat16 [2, 4, 32, 64, 4096], P('gx', 'gy', 'gz'), may hold values from -0.09375 to 0.09375
- point_ids: int32 [2, 4, 32, 64], P('gx', 'gy', 'gz'), may hold values from 0 to 6144, as said below
- theta: float32 [6144], replicated, may hold values from 0.05 to 3.09
- phi: float32 [6144], replicated, may hold values from -3.140625 to 3.140625
Outputs:
- psi4_field: bfloat16 [2, 32, 64, 512], P(None, 'gx', 'gy', 'gz')
- modes: float32 [3, 2, 77], replicated
Inputs may be any that keep to these rules, and one draw needn't show every extreme that they name: `point_ids`: the grid is a window of the extraction region that the spheres cross. A live entry names a sphere point; the value 6144 marks an empty slot, and each list holds its live entries first. The points of sphere s lie in the 9 consecutive block layers along the third dimension that begin at layer s * 10; each point belongs to one column (bx, by) and is listed in exactly two blocks of that column that are adjacent along the third dimension. Some block's list is full, every listing block holds at least 32 live entries, and blocks outside these layers list no point.
All inputs are finite; a program needn't handle non-finite values.
Results may differ from a plain program's by a relative error of at most 0.0032.
Values sent between devices are 32-bit elements; how exact they have to be, the bound alone decides.
No kernel may reach another device: no remote copies, remote signals or barrier semaphores. Data moves between devices by JAX's collectives and lax.ppermute only.
A program may use at most 64 MiB of HBM per device.

v0:
```python
import math
import jax
import jax.numpy as jnp
import numpy as np
from jax import lax
from jax.sharding import PartitionSpec as P

BLK = 16
PB = 64
PTS = 2048
SPHERES = 3
LMAX = 8
PAIRS = [[0, 1, 2], [1, 3, 4], [2, 4, 5]]


def padded_2(cells, sides, width):
    for axis, dim in sides:
        count = lax.axis_size(axis)
        ends = count - 1
        head = lax.slice_in_dim(cells, 0, width, axis=dim)
        tail = lax.slice_in_dim(cells, cells.shape[dim] - width, cells.shape[dim], axis=dim)
        cells = jnp.concatenate(
            [
                lax.ppermute(tail, axis, [(i, (i + 1) % count) for i in range(ends)]),
                cells,
                lax.ppermute(head, axis, [((i + 1) % count, i) for i in range(ends)]),
            ],
            axis=dim,
        )
    return cells


def build_table(degree_max):
    width = 2 * degree_max + 1
    columns = []
    orders = []
    for degree in range(2, degree_max + 1):
        for order in range(-degree, degree + 1):
            column = np.zeros(width * width)
            lead = (-1.0) ** order * math.sqrt(
                math.factorial(degree + order)
                * math.factorial(degree - order)
                * (2 * degree + 1)
                / (4.0 * math.pi * math.factorial(degree - 2) * math.factorial(degree + 2))
            )
            for step in range(0, degree + 3):
                lower = step - 2 - order
                if lower >= 0 and lower <= degree - 2:
                    value = (
                        lead
                        * math.comb(degree + 2, step)
                        * math.comb(degree - 2, lower)
                        * (-1.0) ** (degree - step + 2)
                    )
                    expo = 2 * step - 2 - order
                    column[expo * width + (2 * degree - expo)] += value
            columns.append(column)
            orders.append(order)
    return (np.stack(columns, 1), np.array(orders))


def project(sphere_vals, theta, phi, member):
    table, orders = build_table(LMAX)
    width = 2 * LMAX + 1
    cosine = jnp.cos(theta * 0.5)
    sine = jnp.sin(theta * 0.5)
    cos_pow = jnp.stack([cosine**power for power in range(width)], 1)
    sin_pow = jnp.stack([sine**power for power in range(width)], 1)
    grid_pow = (cos_pow[:, :, None] * sin_pow[:, None, :]).reshape(theta.shape[0], width * width)
    amplitude = jnp.dot(grid_pow, jnp.asarray(table, jnp.float32), precision=lax.Precision.HIGHEST)
    angle_m = phi[:, None] * jnp.asarray(orders, jnp.float32)[None, :]
    y_real = amplitude * jnp.cos(angle_m)
    y_imag = amplitude * jnp.sin(angle_m)
    left_re = member * sphere_vals[0][None, :]
    left_im = member * sphere_vals[1][None, :]
    highest = lax.Precision.HIGHEST
    real = jnp.dot(left_re, y_real, precision=highest) + jnp.dot(left_im, y_imag, precision=highest)
    imag = jnp.dot(left_im, y_real, precision=highest) - jnp.dot(left_re, y_imag, precision=highest)
    return jnp.stack([real, imag], 1) * (4.0 * math.pi / PTS)


def frame_terms(x_coord, y_coord, z_coord):
    x_full = x_coord[:, None, None]
    y_full = y_coord[None, :, None]
    z_full = z_coord[None, None, :]
    radial_xy = jnp.sqrt(x_full * x_full + y_full * y_full)
    radius = jnp.sqrt(radial_xy * radial_xy + z_full * z_full)
    cos_phi = x_full / radial_xy
    sin_phi = y_full / radial_xy
    cos_theta = z_full / radius
    sin_theta = radial_xy / radius
    e_theta = [cos_theta * cos_phi, cos_theta * sin_phi, -sin_theta]
    e_phi = [-sin_phi, cos_phi, 0.0 * cos_phi]
    return (e_theta, e_phi)


def weyl_scalar(padded, x_coord, y_coord, z_coord):
    extent = [x_coord.shape[0], y_coord.shape[0], z_coord.shape[0]]

    def moved(comp, axis, offset):
        index = [slice(2, 2 + count) for count in extent]
        index[axis] = slice(2 + offset, 2 + offset + extent[axis])
        return padded[comp][tuple(index)]

    def first(comp, axis):
        return (
            moved(comp, axis, -2)
            - 8.0 * moved(comp, axis, -1)
            + 8.0 * moved(comp, axis, 1)
            - moved(comp, axis, 2)
        ) / 12.0

    def second(comp, axis):
        return (
            -moved(comp, axis, -2)
            + 16.0 * moved(comp, axis, -1)
            - 30.0 * moved(comp, axis, 0)
            + 16.0 * moved(comp, axis, 1)
            - moved(comp, axis, 2)
        ) / 12.0

    kval = [moved(6 + comp, 0, 0) for comp in range(6)]
    trace = kval[0] + kval[3] + kval[5]
    electric = {}
    for row in range(3):
        for col in range(row, 3):
            comp = PAIRS[row][col]
            laplace = second(comp, 0) + second(comp, 1) + second(comp, 2)
            square = (
                kval[PAIRS[row][0]] * kval[PAIRS[0][col]]
                + kval[PAIRS[row][1]] * kval[PAIRS[1][col]]
                + kval[PAIRS[row][2]] * kval[PAIRS[2][col]]
            )
            value = -0.5 * laplace + trace * kval[comp] - square
            electric[row, col] = value
            electric[col, row] = value
    deriv = [[first(6 + comp, axis) for comp in range(6)] for axis in range(3)]
    curl = {}
    for row in range(3):
        one = (row + 1) % 3
        two = (row + 2) % 3
        for col in range(3):
            curl[row, col] = deriv[one][PAIRS[two][col]] - deriv[two][PAIRS[one][col]]
    e_theta, e_phi = frame_terms(x_coord, y_coord, z_coord)
    real = 0.0
    imag = 0.0
    for row in range(3):
        for col in range(3):
            magnetic = 0.5 * (curl[row, col] + curl[col, row])
            plus = 0.5 * (e_theta[row] * e_theta[col] - e_phi[row] * e_phi[col])
            cross = 0.5 * (e_theta[row] * e_phi[col] + e_phi[row] * e_theta[col])
            real = real + electric[row, col] * plus - magnetic * cross
            imag = imag - electric[row, col] * cross - magnetic * plus
    return jnp.stack([real, imag])


def shards(metric_pert, curvature, interp_weights, point_ids, theta, phi):
    fields = jnp.concatenate([metric_pert, curvature], 0)
    cells_x, cells_y, cells_z = (metric_pert.shape[1], metric_pert.shape[2], metric_pert.shape[3])
    whole_x = cells_x * lax.axis_size("gx")
    whole_y = cells_y * lax.axis_size("gy")
    whole_z = cells_z * lax.axis_size("gz")
    x_coord = (
        (lax.axis_index("gx") * cells_x + jnp.arange(cells_x)).astype(jnp.float32)
        + 0.5
        - whole_x / 2.0
    )
    y_coord = (
        (lax.axis_index("gy") * cells_y + jnp.arange(cells_y)).astype(jnp.float32)
        + 0.5
        - whole_y / 2.0
    )
    z_coord = (
        (lax.axis_index("gz") * cells_z + jnp.arange(cells_z)).astype(jnp.float32)
        + 0.5
        - whole_z / 2.0
    )
    padded = padded_2(fields, (("gx", 1), ("gy", 2), ("gz", 3)), 2)
    psi_local = weyl_scalar(padded, x_coord, y_coord, z_coord).astype(jnp.bfloat16)
    blocks_z = cells_z // BLK
    blocks = (
        psi_local.reshape(2, BLK, BLK, blocks_z, BLK)
        .transpose(3, 0, 1, 2, 4)
        .reshape(blocks_z, 2, BLK * BLK * BLK)
    )
    weights = interp_weights.reshape(blocks_z, PB, BLK * BLK * BLK)
    partial_value = jnp.einsum("bcn,bpn->bpc", blocks, weights, preferred_element_type=jnp.float32)
    slot_values = partial_value.reshape(-1, 2)
    point_list = point_ids.reshape(-1)
    total_points = SPHERES * PTS
    safe_list = jnp.minimum(point_list, total_points - 1)
    member = (point_list[None, :] // PTS == jnp.arange(SPHERES)[:, None]).astype(jnp.float32)
    local_modes = project(slot_values.T, theta[safe_list], phi[safe_list], member)
    modes = lax.psum(local_modes, ("gx", "gy", "gz"))
    return (psi_local, modes)


def solution(mesh):
    in_specs = (
        P(None, "gx", "gy", "gz"),
        P(None, "gx", "gy", "gz"),
        P("gx", "gy", "gz", None, None),
        P("gx", "gy", "gz", None),
        P(),
        P(),
    )
    out_specs = (P(None, "gx", "gy", "gz"), P())
    return jax.shard_map(shards, mesh=mesh, in_specs=in_specs, out_specs=out_specs, check_vma=False)
```

profile of v0, /device:TPU:0, one launch (start us, length us, event | category | flops | bytes accessed | tf_op | source)
XLA Modules:
  0.0 129.0 jit_solution(13485830494498539828)
XLA Ops:
  0.7 1.2 constant_dynamic-update-slice_fusion.1
  1.9 1.2 constant_dynamic-update-slice_fusion
  3.1 0.8 fusion.227
  3.9 4.9 %collective-permute-start = (f32[12,2,16,128]{3,2,1,0:T(8,128)}, f32[12,2,16,128]{3,2,1,0:T(8,128)S(1)}, u32[]{:S(2)}, u32[]{:S(2)}) collective-permute-start(f32[12,2,16,128]{3,2,1,0:T(8,128)} %get-tuple-element.43), channel_id=1, source_target_pairs={{0,16},{1,17},{2,18},{3,19},{4,20},{5,21},{6,22},{7,23},{8,24},{9,... | collective-permute-start | bytes 589832 | tf_op jit(solution)/shard_map/ppermute | solution.py:24
  8.8 1.3 %collective-permute-start.1 = (f32[12,2,16,128]{3,2,1,0:T(8,128)}, f32[12,2,16,128]{3,2,1,0:T(8,128)S(1)}, u32[]{:S(2)}, u32[]{:S(2)}) collective-permute-start(f32[12,2,16,128]{3,2,1,0:T(8,128)} %get-tuple-element.44), channel_id=1, source_target_pairs={{16,0},{17,1},{18,2},{19,3},{20,4},{21,5},{22,6},{23,7},{24,8},{25... | collective-permute-start | bytes 589832 | tf_op jit(solution)/shard_map/ppermute | solution.py:26
  10.8 3.1 %gather_fusion = f32[512]{0:T(512)S(1)} fusion(f32[6144]{0:T(1024)S(1)} %copy-done, s32[1024]{0:T(1024)S(1)} %pad_clamp_fusion), kind=kCustom, calls=%fused_computation | custom fusion | bytes 6144 | tf_op jit(solution)/shard_map/gather | solution.py:193
  14.4 0.7 fusion.167
  15.2 2.0 %collective-permute-done.1 = f32[12,2,16,128]{3,2,1,0:T(8,128)S(1)} collective-permute-done((f32[12,2,16,128]{3,2,1,0:T(8,128)}, f32[12,2,16,128]{3,2,1,0:T(8,128)S(1)}, u32[]{:S(2)}, u32[]{:S(2)}) %collective-permute-start.1) | collective-permute-done | bytes 196640 | tf_op jit(solution)/shard_map/ppermute | solution.py:26
  17.4 1.3 %collective-permute-start.2 = (f32[12,20,2,128]{3,2,1,0:T(2,128)S(1)}, f32[12,20,2,128]{3,2,1,0:T(2,128)S(1)}, u32[]{:S(2)}, u32[]{:S(2)}) collective-permute-start(f32[12,20,2,128]{3,2,1,0:T(2,128)S(1)} %get-tuple-element.41), channel_id=1, source_target_pairs={{0,4},{4,8},{8,12},{1,5},{5,9},{9,13},{2,6},{6,10},{10,14},{3,7},{... | collective-permute-start | bytes 737288 | tf_op jit(solution)/shard_map/ppermute | solution.py:24
  18.7 1.3 %collective-permute-start.3 = (f32[12,20,2,128]{3,2,1,0:T(2,128)S(1)}, f32[12,20,2,128]{3,2,1,0:T(2,128)S(1)}, u32[]{:S(2)}, u32[]{:S(2)}) collective-permute-start(f32[12,20,2,128]{3,2,1,0:T(2,128)S(1)} %get-tuple-element.42), channel_id=1, source_target_pairs={{4,0},{8,4},{12,8},{5,1},{9,5},{13,9},{6,2},{10,6},{14,10},{7,3},{... | collective-permute-start | bytes 737288 | tf_op jit(solution)/shard_map/ppermute | solution.py:26
  20.0 1.6 %fusion.229 = f32[512,77]{0,1:T(8,128)S(1)} fusion(f32[512,289]{0,1:T(8,128)S(1)} %mul.1636, f32[289,77]{1,0:T(8,128)} %constant.111.clone), kind=kOutput, calls=%fused_computation.419 | convolution fusion | flops 136722432 | bytes 838580 | tf_op jit(solution)/shard_map/dot_general | solution.py:70
  21.6 2.3 %collective-permute-done.3 = f32[12,20,2,128]{3,2,1,0:T(2,128)S(1)} collective-permute-done((f32[12,20,2,128]{3,2,1,0:T(2,128)S(1)}, f32[12,20,2,128]{3,2,1,0:T(2,128)S(1)}, u32[]{:S(2)}, u32[]{:S(2)}) %collective-permute-start.3) | collective-permute-done | bytes 245792 | tf_op jit(solution)/shard_map/ppermute | solution.py:26
  23.9 1.4 %pad_maximum_fusion.1 = f32[12,20,20,128]{3,2,1,0:T(8,128)S(1)} fusion(f32[12,20,2,128]{3,2,1,0:T(2,128)S(1)} %collective-permute-done.3, f32[12,2,16,128]{3,2,1,0:T(8,128)} %copy-done.2, f32[12,16,16,128]{3,2,1,0:T(8,128)S(1)} %constant_dynamic-update-slice_fusion, f32[12,2,16,128]{3,2,1,0:T(8,128)S(1)} %collective-permute-done, ...), kind=kLoop, calls=%fused_computation.5 | loop fusion | flops 2457600 | bytes 4915200 | tf_op jit(solution)/shard_map/concatenate | solution.py:22
  25.3 3.5 %fusion.226 = (f32[12,20,20,2]{3,2,1,0:T(8,128)}, f32[12,20,20,2]{3,2,1,0:T(8,128)}) fusion(f32[12,20,20,128]{3,2,1,0:T(8,128)S(1)} %pad_maximum_fusion.1), kind=kLoop, calls=%fused_computation.416 | loop fusion | bytes 153600 | tf_op jit(solution)/shard_map/slice | solution.py:21
  28.8 3.0 %copy.32 = f32[12,20,20,2]{2,3,1,0:T(2,128)S(1)} copy(f32[12,20,20,2]{3,2,1,0:T(8,128)} %get-tuple-element.39) | data formatting | bytes 76800
  31.8 3.5 %collective-permute-start.4 = (f32[12,20,20,2]{2,3,1,0:T(2,128)S(1)}, f32[12,20,20,2]{2,3,1,0:T(2,128)S(1)}, u32[]{:S(2)}, u32[]{:S(2)}) collective-permute-start(f32[12,20,20,2]{2,3,1,0:T(2,128)S(1)} %copy.32), channel_id=1, source_target_pairs={{0,1},{1,2},{2,3},{4,5},{5,6},{6,7},{8,9},{9,10},{10,11},{12,13},{... | collective-permute-start | bytes 115208 | tf_op jit(solution)/shard_map/ppermute | solution.py:24
  35.3 3.0 %copy.33 = f32[12,20,20,2]{2,3,1,0:T(2,128)S(1)} copy(f32[12,20,20,2]{3,2,1,0:T(8,128)} %get-tuple-element.40) | data formatting | bytes 76800
  38.4 1.5 %collective-permute-start.5 = (f32[12,20,20,2]{2,3,1,0:T(2,128)S(1)}, f32[12,20,20,2]{2,3,1,0:T(2,128)}, u32[]{:S(2)}, u32[]{:S(2)}) collective-permute-start(f32[12,20,20,2]{2,3,1,0:T(2,128)S(1)} %copy.33), channel_id=1, source_target_pairs={{1,0},{2,1},{3,2},{5,4},{6,5},{7,6},{9,8},{10,9},{11,10},{13,12},{... | collective-permute-start | bytes 115208 | tf_op jit(solution)/shard_map/ppermute | solution.py:26
  39.9 3.1 %gather_fusion.1 = f32[512]{0:T(512)S(1)} fusion(f32[6144]{0:T(1024)S(1)} %copy-done.1, s32[1024]{0:T(1024)S(1)} %pad_clamp_fusion), kind=kCustom, calls=%fused_computation.1 | custom fusion | bytes 6144 | tf_op jit(solution)/shard_map/gather | solution.py:193
  43.0 2.8 %copy.26 = f32[12,20,20,2]{3,2,1,0:T(8,128)} copy(f32[12,20,20,2]{2,3,1,0:T(2,128)S(1)} %collective-permute-done.4) | data formatting | bytes 76800 | tf_op jit(solution)/shard_map/ppermute | solution.py:24
  46.6 3.7 %copy.27 = f32[12,20,20,2]{3,2,1,0:T(8,128)} copy(f32[12,20,20,2]{2,3,1,0:T(2,128)} %collective-permute-done.5) | data formatting | bytes 76800 | tf_op jit(solution)/shard_map/ppermute | solution.py:26
  50.2 7.0 %pad_maximum_fusion = f32[12,20,20,132]{3,2,1,0:T(8,128)S(1)} fusion(f32[12,20,20,2]{3,2,1,0:T(8,128)} %copy.27, f32[12,20,2,128]{3,2,1,0:T(2,128)S(1)} %collective-permute-done.3, f32[12,2,16,128]{3,2,1,0:T(8,128)S(1)} %copy-done.3, f32[12,16,16,128]{3,2,1,0:T(8,128)S(1)} %constant_dynamic-update-slice_fusion, ...), kind=kLoop, calls=%fused_computation.2 | loop fusion | flops 3801600 | bytes 5068800 | tf_op jit(solution)/shard_map/concatenate | solution.py:22
  57.2 1.8 %slice_bitcast_fusion = (f32[20,20,132]{2,1,0:T(8,128)S(1)}, f32[20,20,132]{2,1,0:T(8,128)S(1)}, f32[20,20,132]{2,1,0:T(8,128)S(1)}, f32[20,20,132]{2,1,0:T(8,12...) fusion(f32[12,20,20,132]{3,2,1,0:T(8,128)S(1)} %pad_maximum_fusion), kind=kLoop, calls=%fused_computation.12 | loop fusion | bytes 5068800 | tf_op jit(solution)/shard_map/squeeze | solution.py:103
  59.0 14.9 %subtract_convert_fusion.1 = (bf16[16,16,128]{2,1,0:T(8,128)(2,1)S(1)}, f32[16,16,128]{2,1,0:T(8,128)S(1)}, f32[16,16,128]{2,1,0:T(8,128)}, f32[16,16,128]{2,1,0...) fusion(f32[16,16]{1,0:T(8,128)S(1)} %get-tuple-element.85, ...), kind=kLoop, calls=%fused_computation.304 | loop fusion | flops 12484608 | bytes 20526080 | tf_op jit(solution)/shard_map/convert.7
  74.0 1.9 %subtract_convert_fusion = bf16[16,16,128]{2,1,0:T(8,128)(2,1)S(1)} fusion(f32[16,16,128]{2,1,0:T(8,128)} %get-tuple-element.26, f32[16,16,128]{2,1,0:T(8,128)} %get-tuple-element.25, f32[16,16,128]{2,1,0:T(8,128)} %get-tuple-element.24, f32[16,16,128]{2,1,0:T(8,128)} %get-tuple-element.23, f32[16,16,128]{2,1,0:T(8,128)} %get-tuple-element.22, ...), kind=kLoop, calls=%fused_computation.303 | loop fusion | flops 2785280 | bytes 1651712 | tf_op jit(solution)/shard_map/convert.6
  77.1 1.1 reshape.879
  78.1 3.4 %fusion.2 = f32[8,64,2]{1,2,0:T(2,128)S(1)} fusion(bf16[8,2,4096]{2,1,0:T(2,128)(2,1)S(1)} %reshape.879, bf16[1,1,8,64,4096]{4,3,2,1,0:T(8,128)(2,1)} %param.10), kind=kOutput, calls=%fused_computation.6 | convolution fusion | flops 8388608 | bytes 4329472 | tf_op jit(solution)/shard_map/bcn,bpn->bpc/dot_general | solution.py:187
  81.6 0.8 fusion.13
  82.4 0.8 fusion.11
  83.2 0.8 fusion.6
  84.1 0.8 fusion.5
  85.0 42.8 %psum.7 = f32[3,2,77]{2,0,1:T(4,128)S(1)} all-reduce(f32[3,2,77]{2,0,1:T(4,128)S(1)} %maximum_multiply_fusion), channel_id=1, replica_groups=mesh['gx'=2,'gy'=4,'gz'=4] {'gx','gy','gz'}, use_global_device_ids=true, to_apply=%region_0.1 | all-reduce | flops 462 | bytes 3696 | tf_op jit(solution)/shard_map/psum | solution.py:194
  (45 shorter events, 4.5 us)
Async XLA Ops:
  0.6 10.2 %copy-start = (f32[6144]{0:T(1024)S(1)}, f32[6144]{0:T(1024)}, u32[]{:S(2)}) copy-start(f32[6144]{0:T(1024)} %param.12) | copy-start | bytes 73732
  0.6 9.4 %copy-start.4 = (s32[1,1,8,64]{3,2,1,0:T(8,128)S(1)}, s32[1,1,8,64]{3,2,1,0:T(8,128)}, u32[]{:S(2)}) copy-start(s32[1,1,8,64]{3,2,1,0:T(8,128)} %param.11) | copy-start | bytes 6148
  3.9 11.3 %collective-permute-start = (f32[12,2,16,128]{3,2,1,0:T(8,128)}, f32[12,2,16,128]{3,2,1,0:T(8,128)S(1)}, u32[]{:S(2)}, u32[]{:S(2)}) collective-permute-start(f32[12,2,16,128]{3,2,1,0:T(8,128)} %get-tuple-element.43), channel_id=1, source_target_pairs={{0,16},{1,17},{2,18},{3,19},{4,20},{5,21},{6,22},{7,23},{8,24},{9,... | collective-permute-start | bytes 589832 | tf_op jit(solution)/shard_map/ppermute | solution.py:24
  8.8 8.5 %collective-permute-start.1 = (f32[12,2,16,128]{3,2,1,0:T(8,128)}, f32[12,2,16,128]{3,2,1,0:T(8,128)S(1)}, u32[]{:S(2)}, u32[]{:S(2)}) collective-permute-start(f32[12,2,16,128]{3,2,1,0:T(8,128)} %get-tuple-element.44), channel_id=1, source_target_pairs={{16,0},{17,1},{18,2},{19,3},{20,4},{21,5},{22,6},{23,7},{24,8},{25... | collective-permute-start | bytes 589832 | tf_op jit(solution)/shard_map/ppermute | solution.py:26
  17.2 1.5 %copy-start.2 = (f32[12,2,16,128]{3,2,1,0:T(8,128)}, f32[12,2,16,128]{3,2,1,0:T(8,128)S(1)}, u32[]{:S(2)}) copy-start(f32[12,2,16,128]{3,2,1,0:T(8,128)S(1)} %collective-permute-done.1) | copy-start | bytes 589828
  17.4 4.2 %collective-permute-start.2 = (f32[12,20,2,128]{3,2,1,0:T(2,128)S(1)}, f32[12,20,2,128]{3,2,1,0:T(2,128)S(1)}, u32[]{:S(2)}, u32[]{:S(2)}) collective-permute-start(f32[12,20,2,128]{3,2,1,0:T(2,128)S(1)} %get-tuple-element.41), channel_id=1, source_target_pairs={{0,4},{4,8},{8,12},{1,5},{5,9},{9,13},{2,6},{6,10},{10,14},{3,7},{... | collective-permute-start | bytes 737288 | tf_op jit(solution)/shard_map/ppermute | solution.py:24
  18.7 5.1 %collective-permute-start.3 = (f32[12,20,2,128]{3,2,1,0:T(2,128)S(1)}, f32[12,20,2,128]{3,2,1,0:T(2,128)S(1)}, u32[]{:S(2)}, u32[]{:S(2)}) collective-permute-start(f32[12,20,2,128]{3,2,1,0:T(2,128)S(1)} %get-tuple-element.42), channel_id=1, source_target_pairs={{4,0},{8,4},{12,8},{5,1},{9,5},{13,9},{6,2},{10,6},{14,10},{7,3},{... | collective-permute-start | bytes 737288 | tf_op jit(solution)/shard_map/ppermute | solution.py:26
  28.8 11.1 %copy-start.1 = (f32[6144]{0:T(1024)S(1)}, f32[6144]{0:T(1024)}, u32[]{:S(2)}) copy-start(f32[6144]{0:T(1024)} %param.13) | copy-start | bytes 73732
  31.8 11.2 %collective-permute-start.4 = (f32[12,20,20,2]{2,3,1,0:T(2,128)S(1)}, f32[12,20,20,2]{2,3,1,0:T(2,128)S(1)}, u32[]{:S(2)}, u32[]{:S(2)}) collective-permute-start(f32[12,20,20,2]{2,3,1,0:T(2,128)S(1)} %copy.32), channel_id=1, source_target_pairs={{0,1},{1,2},{2,3},{4,5},{5,6},{6,7},{8,9},{9,10},{10,11},{12,13},{... | collective-permute-start | bytes 115208 | tf_op jit(solution)/shard_map/ppermute | solution.py:24
  38.4 8.2 %collective-permute-start.5 = (f32[12,20,20,2]{2,3,1,0:T(2,128)S(1)}, f32[12,20,20,2]{2,3,1,0:T(2,128)}, u32[]{:S(2)}, u32[]{:S(2)}) collective-permute-start(f32[12,20,20,2]{2,3,1,0:T(2,128)S(1)} %copy.33), channel_id=1, source_target_pairs={{1,0},{2,1},{3,2},{5,4},{6,5},{7,6},{9,8},{10,9},{11,10},{13,12},{... | collective-permute-start | bytes 115208 | tf_op jit(solution)/shard_map/ppermute | solution.py:26
  43.0 7.2 %copy-start.3 = (f32[12,2,16,128]{3,2,1,0:T(8,128)S(1)}, f32[12,2,16,128]{3,2,1,0:T(8,128)}, u32[]{:S(2)}) copy-start(f32[12,2,16,128]{3,2,1,0:T(8,128)} %copy-done.2) | copy-start | bytes 589828
  77.0 4.6 %copy-start.5 = (f32[77]{0:T(128)S(1)}, f32[77]{0:T(128)}, u32[]{:S(2)}) copy-start(f32[77]{0:T(128)} %constant.112.clone) | copy-start | bytes 928
where the time goes:
time: 130 us; the launch traced here: 129 us
  blocking collectives  42.8 us (33%)
  local copies, waits for them, and re-layouts  30.5 us (23%)
  other arithmetic  27.8 us (21%)
  starting transfers between devices  13.7 us (11%)
  matrix products  8.25 us (6%)
  waiting for transfers between devices  4.98 us (4%)
    psum x1, blocking collectives, shards(): modes = lax.psum(local_modes, ('gx', 'gy', 'gz'))  42.8 us
    another operation x2, other arithmetic  16.9 us
    ppermute x3, starting transfers between devices, padded_2(): lax.ppermute(tail, axis, [(i, (i + 1) % count) for i in range(ends)])  9.67 us
    concatenate x2, other arithmetic, padded_2(): jnp.concatenate([lax.ppermute(tail, axis, [(i, (i + 1) % count) for i in...  8.35 us
    unnamed x16, local copies, waits for them, and re-layouts  7.91 us
    ppermute x3, waiting for transfers between devices, padded_2(): lax.ppermute(head, axis, [((i + 1) % count, i) for i in range(ends)])  4.97 us
    slice x2, local copies, waits for them, and re-layouts, padded_2(): lax.slice_in_dim(cells, cells.shape[dim] - width, cells.shape[dim], axis=...  4.32 us
    ppermute x3, starting transfers between devices, padded_2(): lax.ppermute(head, axis, [((i + 1) % count, i) for i in range(ends)])  4.06 us
  transfers between devices with their start and end apart: 6, of which 3 were waited for; matrix products, arithmetic and copies ran while one was open for 12% of the time, Pallas kernels for 0%

commit v1 on v0

--- a/solution.py
+++ b/solution.py
@@ -191,7 +191,7 @@
     safe_list = jnp.minimum(point_list, total_points - 1)
     member = (point_list[None, :] // PTS == jnp.arange(SPHERES)[:, None]).astype(jnp.float32)
     local_modes = project(slot_values.T, theta[safe_list], phi[safe_list], member)
-    modes = lax.psum(local_modes, ("gx", "gy", "gz"))
+    modes = jnp.sum(lax.all_gather(local_modes, ("gx", "gy", "gz")), 0)
     return (psi_local, modes)
 
 

time: 130 us -> 155 us (1.19)
  blocking collectives: 42.8 us -> 68.1 us
    all_gather x0 -> x1, blocking collectives: none -> 68.1 us  [shards(): modes = jnp.sum(lax.all_gather(local_modes, ('gx', 'gy', 'gz')), 0)]
    psum x1 -> x0, blocking collectives: 42.8 us -> none  [shards(): modes = lax.psum(local_modes, ('gx', 'gy', 'gz'))]
    unnamed x16 -> x15, local copies, waits for them, and re-layouts: 7.91 us -> 7.33 us
  transfers between devices with their start and end apart: 6 -> 6, of which waited for: 3 -> 3; matrix products, arithmetic and copies ran while one was open for 12% -> 10% of each run, Pallas kernels for 0% -> 0%
where the time goes in v1:
time: 155 us; the launch traced here: 154 us
  blocking collectives  68.1 us (44%)
  local copies, waits for them, and re-layouts  29.9 us (19%)
  other arithmetic  28.4 us (18%)
  starting transfers between devices  13.7 us (9%)
  matrix products  8.25 us (5%)
  waiting for transfers between devices  4.98 us (3%)
    all_gather x1, blocking collectives, shards(): modes = jnp.sum(lax.all_gather(local_modes, ('gx', 'gy', 'gz')), 0)  68.1 us
    another operation x2, other arithmetic  16.9 us
    ppermute x3, starting transfers between devices, padded_2(): lax.ppermute(tail, axis, [(i, (i + 1) % count) for i in range(ends)])  9.67 us
    concatenate x2, other arithmetic, padded_2(): jnp.concatenate([lax.ppermute(tail, axis, [(i, (i + 1) % count) for i in...  8.35 us
    unnamed x15, local copies, waits for them, and re-layouts  7.33 us
    ppermute x3, waiting for transfers between devices, padded_2(): lax.ppermute(head, axis, [((i + 1) % count, i) for i in range(ends)])  4.97 us
    slice x2, local copies, waits for them, and re-layouts, padded_2(): lax.slice_in_dim(cells, cells.shape[dim] - width, cells.shape[dim], axis=...  4.32 us
    ppermute x3, starting transfers between devices, padded_2(): lax.ppermute(head, axis, [((i + 1) % count, i) for i in range(ends)])  4.06 us
  transfers between devices with their start and end apart: 6, of which 3 were waited for; matrix products, arithmetic and copies ran while one was open for 10% of the time, Pallas kernels for 0%

profile of v1, /device:TPU:0, one launch (start us, length us, event | category | flops | bytes accessed | tf_op | source)
XLA Modules:
  0.0 154.4 jit_solution(15635720790880607436)
XLA Ops:
  0.7 1.2 constant_dynamic-update-slice_fusion.1
  1.9 1.2 constant_dynamic-update-slice_fusion
  3.1 0.8 fusion.227
  3.9 4.9 %collective-permute-start = (f32[12,2,16,128]{3,2,1,0:T(8,128)}, f32[12,2,16,128]{3,2,1,0:T(8,128)S(1)}, u32[]{:S(2)}, u32[]{:S(2)}) collective-permute-start(f32[12,2,16,128]{3,2,1,0:T(8,128)} %get-tuple-element.39), channel_id=1, source_target_pairs={{0,16},{1,17},{2,18},{3,19},{4,20},{5,21},{6,22},{7,23},{8,24},{9,... | collective-permute-start | bytes 589832 | tf_op jit(solution)/shard_map/ppermute | solution.py:24
  8.8 1.3 collective-permute-start.1
  10.8 3.1 %gather_fusion = f32[512]{0:T(512)S(1)} fusion(f32[6144]{0:T(1024)S(1)} %copy-done, s32[1024]{0:T(1024)S(1)} %pad_clamp_fusion), kind=kCustom, calls=%fused_computation | custom fusion | bytes 6144 | tf_op jit(solution)/shard_map/gather | solution.py:193
  14.4 0.7 fusion.167
  15.2 2.0 %collective-permute-done.1 = f32[12,2,16,128]{3,2,1,0:T(8,128)S(1)} collective-permute-done((f32[12,2,16,128]{3,2,1,0:T(8,128)}, f32[12,2,16,128]{3,2,1,0:T(8,128)S(1)}, u32[]{:S(2)}, u32[]{:S(2)}) %collective-permute-start.1) | collective-permute-done | bytes 196640 | tf_op jit(solution)/shard_map/ppermute | solution.py:26
  17.4 1.3 collective-permute-start.2
  18.7 1.3 collective-permute-start.3
  20.0 1.6 %fusion.229 = f32[512,77]{0,1:T(8,128)S(1)} fusion(f32[512,289]{0,1:T(8,128)S(1)} %mul.1643, f32[289,77]{1,0:T(8,128)} %constant.112.clone), kind=kOutput, calls=%fused_computation.419 | convolution fusion | flops 136722432 | bytes 838580 | tf_op jit(solution)/shard_map/dot_general | solution.py:70
  21.6 2.3 %collective-permute-done.3 = f32[12,20,2,128]{3,2,1,0:T(2,128)S(1)} collective-permute-done((f32[12,20,2,128]{3,2,1,0:T(2,128)S(1)}, f32[12,20,2,128]{3,2,1,0:T(2,128)S(1)}, u32[]{:S(2)}, u32[]{:S(2)}) %collective-permute-start.3) | collective-permute-done | bytes 245792 | tf_op jit(solution)/shard_map/ppermute | solution.py:26
  23.9 1.4 pad_maximum_fusion.1
  25.3 3.5 %fusion.226 = (f32[12,20,20,2]{3,2,1,0:T(8,128)}, f32[12,20,20,2]{3,2,1,0:T(8,128)}) fusion(f32[12,20,20,128]{3,2,1,0:T(8,128)S(1)} %pad_maximum_fusion.1), kind=kLoop, calls=%fused_computation.416 | loop fusion | bytes 153600 | tf_op jit(solution)/shard_map/slice | solution.py:21
  28.8 3.0 %copy.35 = f32[12,20,20,2]{2,3,1,0:T(2,128)S(1)} copy(f32[12,20,20,2]{3,2,1,0:T(8,128)} %get-tuple-element.35) | data formatting | bytes 76800
  31.8 3.5 %collective-permute-start.4 = (f32[12,20,20,2]{2,3,1,0:T(2,128)S(1)}, f32[12,20,20,2]{2,3,1,0:T(2,128)S(1)}, u32[]{:S(2)}, u32[]{:S(2)}) collective-permute-start(f32[12,20,20,2]{2,3,1,0:T(2,128)S(1)} %copy.35), channel_id=1, source_target_pairs={{0,1},{1,2},{2,3},{4,5},{5,6},{6,7},{8,9},{9,10},{10,11},{12,13},{... | collective-permute-start | bytes 115208 | tf_op jit(solution)/shard_map/ppermute | solution.py:24
  35.3 3.0 %copy.36 = f32[12,20,20,2]{2,3,1,0:T(2,128)S(1)} copy(f32[12,20,20,2]{3,2,1,0:T(8,128)} %get-tuple-element.36) | data formatting | bytes 76800
  38.4 1.5 collective-permute-start.5
  39.9 3.1 %gather_fusion.1 = f32[512]{0:T(512)S(1)} fusion(f32[6144]{0:T(1024)S(1)} %copy-done.1, s32[1024]{0:T(1024)S(1)} %pad_clamp_fusion), kind=kCustom, calls=%fused_computation.1 | custom fusion | bytes 6144 | tf_op jit(solution)/shard_map/gather | solution.py:193
  43.0 2.8 %copy.26 = f32[12,20,20,2]{3,2,1,0:T(8,128)} copy(f32[12,20,20,2]{2,3,1,0:T(2,128)S(1)} %collective-permute-done.4) | data formatting | bytes 76800 | tf_op jit(solution)/shard_map/ppermute | solution.py:24
  46.6 3.7 %copy.27 = f32[12,20,20,2]{3,2,1,0:T(8,128)} copy(f32[12,20,20,2]{2,3,1,0:T(2,128)} %collective-permute-done.5) | data formatting | bytes 76800 | tf_op jit(solution)/shard_map/ppermute | solution.py:26
  50.2 7.0 %pad_maximum_fusion = f32[12,20,20,132]{3,2,1,0:T(8,128)S(1)} fusion(f32[12,20,20,2]{3,2,1,0:T(8,128)} %copy.27, f32[12,20,2,128]{3,2,1,0:T(2,128)S(1)} %collective-permute-done.3, f32[12,2,16,128]{3,2,1,0:T(8,128)S(1)} %copy-done.3, f32[12,16,16,128]{3,2,1,0:T(8,128)S(1)} %constant_dynamic-update-slice_fusion, ...), kind=kLoop, calls=%fused_computation.2 | loop fusion | flops 3801600 | bytes 5068800 | tf_op jit(solution)/shard_map/concatenate | solution.py:22
  57.2 1.8 %slice_bitcast_fusion = (f32[20,20,132]{2,1,0:T(8,128)S(1)}, f32[20,20,132]{2,1,0:T(8,128)S(1)}, f32[20,20,132]{2,1,0:T(8,128)S(1)}, f32[20,20,132]{2,1,0:T(8,12...) fusion(f32[12,20,20,132]{3,2,1,0:T(8,128)S(1)} %pad_maximum_fusion), kind=kLoop, calls=%fused_computation.12 | loop fusion | bytes 5068800 | tf_op jit(solution)/shard_map/squeeze | solution.py:103
  59.0 14.9 %subtract_convert_fusion.1 = (bf16[16,16,128]{2,1,0:T(8,128)(2,1)S(1)}, f32[16,16,128]{2,1,0:T(8,128)S(1)}, f32[16,16,128]{2,1,0:T(8,128)}, f32[16,16,128]{2,1,0...) fusion(f32[16,16]{1,0:T(8,128)S(1)} %get-tuple-element.81, ...), kind=kLoop, calls=%fused_computation.304 | loop fusion | flops 12484608 | bytes 20526080 | tf_op jit(solution)/shard_map/convert.7
  74.0 1.9 %subtract_convert_fusion = bf16[16,16,128]{2,1,0:T(8,128)(2,1)S(1)} fusion(f32[16,16,128]{2,1,0:T(8,128)} %get-tuple-element.22, f32[16,16,128]{2,1,0:T(8,128)} %get-tuple-element.21, f32[16,16,128]{2,1,0:T(8,128)} %get-tuple-element.20, f32[16,16,128]{2,1,0:T(8,128)} %get-tuple-element.19, f32[16,16,128]{2,1,0:T(8,128)} %get-tuple-element.18, ...), kind=kLoop, calls=%fused_computation.303 | loop fusion | flops 2785280 | bytes 1651712 | tf_op jit(solution)/shard_map/convert.6
  77.1 1.1 reshape.910
  78.1 3.4 %fusion.2 = f32[8,64,2]{1,2,0:T(2,128)S(1)} fusion(bf16[8,2,4096]{2,1,0:T(2,128)(2,1)S(1)} %reshape.910, bf16[1,1,8,64,4096]{4,3,2,1,0:T(8,128)(2,1)} %param.10), kind=kOutput, calls=%fused_computation.6 | convolution fusion | flops 8388608 | bytes 4329472 | tf_op jit(solution)/shard_map/bcn,bpn->bpc/dot_general | solution.py:187
  81.6 0.8 fusion.13
  82.4 0.8 fusion.11
  83.2 0.8 fusion.6
  84.1 0.8 fusion.5
  85.0 68.1 %all_gather.4 = f32[32,3,2,77]{3,2,1,0:T(2,128)S(1)} all-gather(f32[1,3,2,77]{3,2,1,0:T(2,128)S(1)} %copy.31), channel_id=1, replica_groups=mesh['gx'=2,'gy'=4,'gz'=4] {'gx','gy','gz'}, dimensions={0}, use_global_device_ids=true | all-gather | bytes 60984 | tf_op jit(solution)/shard_map/all_gather | solution.py:194
  (46 shorter events, 4.6 us)
Async XLA Ops:
  0.6 10.2 %copy-start = (f32[6144]{0:T(1024)S(1)}, f32[6144]{0:T(1024)}, u32[]{:S(2)}) copy-start(f32[6144]{0:T(1024)} %param.12) | copy-start | bytes 73732
  0.6 9.4 %copy-start.4 = (s32[1,1,8,64]{3,2,1,0:T(8,128)S(1)}, s32[1,1,8,64]{3,2,1,0:T(8,128)}, u32[]{:S(2)}) copy-start(s32[1,1,8,64]{3,2,1,0:T(8,128)} %param.11) | copy-start | bytes 6148
  3.9 11.3 %collective-permute-start = (f32[12,2,16,128]{3,2,1,0:T(8,128)}, f32[12,2,16,128]{3,2,1,0:T(8,128)S(1)}, u32[]{:S(2)}, u32[]{:S(2)}) collective-permute-start(f32[12,2,16,128]{3,2,1,0:T(8,128)} %get-tuple-element.39), channel_id=1, source_target_pairs={{0,16},{1,17},{2,18},{3,19},{4,20},{5,21},{6,22},{7,23},{8,24},{9,... | collective-permute-start | bytes 589832 | tf_op jit(solution)/shard_map/ppermute | solution.py:24
  8.8 8.5 %collective-permute-start.1 = (f32[12,2,16,128]{3,2,1,0:T(8,128)}, f32[12,2,16,128]{3,2,1,0:T(8,128)S(1)}, u32[]{:S(2)}, u32[]{:S(2)}) collective-permute-start(f32[12,2,16,128]{3,2,1,0:T(8,128)} %get-tuple-element.40), channel_id=1, source_target_pairs={{16,0},{17,1},{18,2},{19,3},{20,4},{21,5},{22,6},{23,7},{24,8},{25... | collective-permute-start | bytes 589832 | tf_op jit(solution)/shard_map/ppermute | solution.py:26
  17.2 1.5 copy-start.2
  17.4 4.2 %collective-permute-start.2 = (f32[12,20,2,128]{3,2,1,0:T(2,128)S(1)}, f32[12,20,2,128]{3,2,1,0:T(2,128)S(1)}, u32[]{:S(2)}, u32[]{:S(2)}) collective-permute-start(f32[12,20,2,128]{3,2,1,0:T(2,128)S(1)} %get-tuple-element.37), channel_id=1, source_target_pairs={{0,4},{4,8},{8,12},{1,5},{5,9},{9,13},{2,6},{6,10},{10,14},{3,7},{... | collective-permute-start | bytes 737288 | tf_op jit(solution)/shard_map/ppermute | solution.py:24
  18.7 5.1 %collective-permute-start.3 = (f32[12,20,2,128]{3,2,1,0:T(2,128)S(1)}, f32[12,20,2,128]{3,2,1,0:T(2,128)S(1)}, u32[]{:S(2)}, u32[]{:S(2)}) collective-permute-start(f32[12,20,2,128]{3,2,1,0:T(2,128)S(1)} %get-tuple-element.38), channel_id=1, source_target_pairs={{4,0},{8,4},{12,8},{5,1},{9,5},{13,9},{6,2},{10,6},{14,10},{7,3},{... | collective-permute-start | bytes 737288 | tf_op jit(solution)/shard_map/ppermute | solution.py:26
  28.8 11.1 %copy-start.1 = (f32[6144]{0:T(1024)S(1)}, f32[6144]{0:T(1024)}, u32[]{:S(2)}) copy-start(f32[6144]{0:T(1024)} %param.13) | copy-start | bytes 73732
  31.8 11.2 %collective-permute-start.4 = (f32[12,20,20,2]{2,3,1,0:T(2,128)S(1)}, f32[12,20,20,2]{2,3,1,0:T(2,128)S(1)}, u32[]{:S(2)}, u32[]{:S(2)}) collective-permute-start(f32[12,20,20,2]{2,3,1,0:T(2,128)S(1)} %copy.35), channel_id=1, source_target_pairs={{0,1},{1,2},{2,3},{4,5},{5,6},{6,7},{8,9},{9,10},{10,11},{12,13},{... | collective-permute-start | bytes 115208 | tf_op jit(solution)/shard_map/ppermute | solution.py:24
  38.4 8.2 %collective-permute-start.5 = (f32[12,20,20,2]{2,3,1,0:T(2,128)S(1)}, f32[12,20,20,2]{2,3,1,0:T(2,128)}, u32[]{:S(2)}, u32[]{:S(2)}) collective-permute-start(f32[12,20,20,2]{2,3,1,0:T(2,128)S(1)} %copy.36), channel_id=1, source_target_pairs={{1,0},{2,1},{3,2},{5,4},{6,5},{7,6},{9,8},{10,9},{11,10},{13,12},{... | collective-permute-start | bytes 115208 | tf_op jit(solution)/shard_map/ppermute | solution.py:26
  43.0 7.2 %copy-start.3 = (f32[12,2,16,128]{3,2,1,0:T(8,128)S(1)}, f32[12,2,16,128]{3,2,1,0:T(8,128)}, u32[]{:S(2)}) copy-start(f32[12,2,16,128]{3,2,1,0:T(8,128)} %copy-done.2) | copy-start | bytes 589828
  77.0 4.6 %copy-start.5 = (f32[77]{0:T(128)S(1)}, f32[77]{0:T(128)}, u32[]{:S(2)}) copy-start(f32[77]{0:T(128)} %constant.113.clone) | copy-start | bytes 928
